TPU v7x, 128 devices: a whole 4x4x4 slice. The times are simulated.
128 devices in a mesh: ka: 16 (over y, z), row: 8 (over x, core).
Axes of the slice: x: 4, y: 4, z: 4, core: 2. Of those that a mesh axis runs over, the one named last changes fastest.
Arguments:
- base_k: float32 [128, 3], P('ka'), may hold values from 0 to 1
- counts: int32 [128], P('ka'), may hold values from 1 to 4, 320 in all
- block_order: int32 [128], P(('ka', 'row')), may hold values from 0 to 127, each once
- lattice: int32 [4096, 3], P('row'), may hold values from -8 to 7, as said below
- real_space: bfloat16 [4096, 3, 128, 2, 128], P('row', None, 'ka'), may hold values from -0.09375 to 0.09375
- eigvecs: bfloat16 [512, 128, 2, 128], P(('ka', 'row')), may hold values from -0.5 to 0.5
- occupied: int32 [512, 128], P(('ka', 'row')), may hold values 0 or 1
Outputs:
- curvature: float32 [512], P(('ka', 'row'))
Inputs may be any that keep to these rules, and one draw needn't show every extreme that they name: The counts sum to 320, and some block has count 4. `block_order`: each block stands at exactly one position. `lattice`: all 4096 R-vectors are distinct.
All inputs are finite; a program needn't handle non-finite values. No bound on the sum of `occupied` on one device may be relied on, other than what follows from the above.
Results may differ from a plain program's by a relative error of at most 0.012.
The roundings to bfloat16 on the way count: a program that leaves them out, or rounds other values in their place, can miss the bound.
Values sent between devices are 32-bit elements; how exact they have to be, the bound alone decides.
No kernel may reach another device: no remote copies, remote signals or barrier semaphores. Data moves between devices by JAX's collectives and lax.ppermute only.
A program may use at most 128 MiB of HBM per device.

v0:
```python
import math
import jax
import jax.numpy as jnp
from jax import lax
from jax.sharding import Mesh
from jax.sharding import PartitionSpec as P

SUB = 4
KA = ("ka_0", "ka_1")
KA_ROW = ("ka_0", "ka_1", "row_0", "row_1")
ROW = ("row_0", "row_1")
broadening = 1.0
refine_step = (0.05, 0.03, 0.02)


def sent_to_all(value, axis):
    copies = jnp.broadcast_to(value, (lax.axis_size(axis), *value.shape))
    return lax.all_to_all(copies, axis, split_axis=0, concat_axis=0, tiled=True)


def laid_out(pieces, dim):
    lengths = list(pieces.shape[1:])
    lengths[dim] *= pieces.shape[0]
    return jnp.moveaxis(pieces, 0, dim).reshape(lengths)


def gather_directly(value, axis, dim):
    pieces = sent_to_all(value, axis)
    return laid_out(pieces, dim)


def gather_in_order(value, axes, sequence):
    pieces = value[None]
    for k in sequence:
        pieces = lax.all_gather(pieces, axes[k], axis=0, tiled=True)
    held = [lax.axis_size(axes[k]) for k in reversed(sequence)]
    pieces = pieces.reshape(*held, *value.shape)
    turned = sorted(range(len(sequence)), key=lambda place: sequence[len(sequence) - 1 - place])
    return pieces.transpose(*turned, *range(len(sequence), pieces.ndim)).reshape(-1, *value.shape)


def gathered_by_axis(value, axes, sequence, dim):
    return laid_out(gather_in_order(value, axes, sequence), dim)


def slot_points(base_points, block_counts):
    count_float = block_counts.astype(jnp.float32)
    sub_index = jnp.arange(SUB, dtype=jnp.float32)
    fraction = (sub_index[None, :] + 0.5) / count_float[:, None] - 0.5
    refine = jnp.array(refine_step, dtype=jnp.float32)
    kpoints = base_points[:, None, :] + fraction[:, :, None] * refine[None, None, :]
    alive = jnp.arange(SUB, dtype=jnp.int32)[None, :] < block_counts[:, None]
    weight = jnp.where(alive, 1.0 / count_float[:, None], 0.0)
    block_total = base_points.shape[0]
    return (kpoints.reshape(block_total * SUB, 3), weight.reshape(block_total * SUB))


def make_phases(kpoints, lattice):
    coords = lattice.astype(jnp.float32)
    angles = (
        2.0
        * math.pi
        * (
            kpoints[:, 0:1] * coords[None, :, 0]
            + kpoints[:, 1:2] * coords[None, :, 1]
            + kpoints[:, 2:3] * coords[None, :, 2]
        )
    )
    cosines = jnp.cos(angles)
    sines = jnp.sin(angles)
    coord_x = coords[None, :, 0]
    coord_y = coords[None, :, 1]
    return jnp.stack(
        [cosines, sines, -coord_x * sines, coord_x * cosines, -coord_y * sines, coord_y * cosines]
    ).astype(jnp.bfloat16)


def combine(first_part, second_part):
    real_part = first_part[..., 0, :] - second_part[..., 1, :]
    imag_part = second_part[..., 0, :] + first_part[..., 1, :]
    return jnp.stack([real_part, imag_part], axis=-2)


def fourier(kpoints, lattice, real_space):
    phase_rows = make_phases(kpoints, lattice)
    row_count = kpoints.shape[0]
    r_count = real_space.shape[0]
    slab_rows = real_space.shape[2]
    width = real_space.shape[4]
    matrix_h = real_space[:, 0].reshape(r_count, slab_rows * 2 * width)
    matrix_a = real_space[:, 1:3].reshape(r_count, 2 * slab_rows * 2 * width)
    product_h = jnp.dot(
        phase_rows.reshape(6 * row_count, r_count), matrix_h, preferred_element_type=jnp.float32
    ).reshape(6, row_count, slab_rows, 2, width)
    product_a = jnp.dot(
        phase_rows[0:2].reshape(2 * row_count, r_count),
        matrix_a,
        preferred_element_type=jnp.float32,
    ).reshape(2, row_count, 2, slab_rows, 2, width)
    pieces = [
        combine(product_h[0], product_h[1]),
        combine(product_h[2], product_h[3]),
        combine(product_h[4], product_h[5]),
        combine(product_a[0, :, 0], product_a[1, :, 0]),
        combine(product_a[0, :, 1], product_a[1, :, 1]),
    ]
    return jnp.stack(pieces, axis=1)


def curvature(k_field, vectors, occupied, weight):
    best = lax.Precision.HIGHEST
    width = k_field.shape[-1]
    vectors_f = vectors.astype(jnp.float32)
    mat_real = k_field[:, :, :, 0, :]
    mat_imag = k_field[:, :, :, 1, :]
    vec_real = vectors_f[:, :, 0, :]
    vec_imag = vectors_f[:, :, 1, :]
    turned_real = jnp.einsum("ncij,njb->ncib", mat_real, vec_real, precision=best) - jnp.einsum(
        "ncij,njb->ncib", mat_imag, vec_imag, precision=best
    )
    turned_imag = jnp.einsum("ncij,njb->ncib", mat_real, vec_imag, precision=best) + jnp.einsum(
        "ncij,njb->ncib", mat_imag, vec_real, precision=best
    )
    energy = jnp.sum(vec_real * turned_real[:, 0] + vec_imag * turned_imag[:, 0], axis=1)
    bar_real = jnp.einsum(
        "nia,ncib->ncab", vec_real, turned_real[:, 1:], precision=best
    ) + jnp.einsum("nia,ncib->ncab", vec_imag, turned_imag[:, 1:], precision=best)
    bar_imag = jnp.einsum(
        "nia,ncib->ncab", vec_real, turned_imag[:, 1:], precision=best
    ) - jnp.einsum("nia,ncib->ncab", vec_imag, turned_real[:, 1:], precision=best)
    spacing = energy[:, None, :] - energy[:, :, None]
    smoothed = spacing / (spacing * spacing + broadening)
    xcov_real = bar_real[:, 2] + smoothed * bar_real[:, 0]
    xcov_imag = bar_imag[:, 2] + smoothed * bar_imag[:, 0]
    ycov_real = bar_real[:, 3] + smoothed * bar_real[:, 1]
    ycov_imag = bar_imag[:, 3] + smoothed * bar_imag[:, 1]
    product_im = xcov_real * jnp.swapaxes(ycov_imag, 1, 2) + xcov_imag * jnp.swapaxes(
        ycov_real, 1, 2
    )
    filled = occupied.astype(jnp.float32)
    pairing = filled[:, :, None] * (1.0 - filled[:, None, :])
    berry_sum = -2.0 / width * jnp.sum(pairing * product_im, axis=(1, 2))
    return weight * berry_sum


def on_device(base_k, counts, block_order, lattice, real_space, eigvecs, occupied):
    all_base, all_counts = (gather_directly(base_k, KA, 0), gather_directly(counts, KA, 0))
    all_order = gathered_by_axis(block_order, (("ka_0", "ka_1", "row_0"), "row_1"), (0, 1), 0)
    block_total = all_order.shape[0]
    chosen = all_order[:, None] == jnp.arange(block_total, dtype=jnp.int32)[None, :]
    block_counts = jnp.sum(jnp.where(chosen, all_counts[None, :], 0), axis=1).astype(jnp.int32)
    base_points = jnp.sum(jnp.where(chosen[:, :, None], all_base[None, :, :], 0.0), axis=1)
    kpoints, weight = slot_points(base_points, block_counts)
    slot_count = kpoints.shape[0]
    ka_size = lax.axis_size(KA)
    row_size = lax.axis_size(ROW)
    per_device = slot_count // (ka_size * row_size)
    width = real_space.shape[4]
    slot_order = (
        jnp.arange(slot_count, dtype=jnp.int32)
        .reshape(ka_size, row_size, per_device)
        .transpose(1, 0, 2)
        .reshape(slot_count)
    )
    summed = lax.psum_scatter(
        fourier(kpoints[slot_order], lattice, real_space), ROW, scatter_dimension=0, tiled=True
    )
    reduced = summed.reshape((ka_size, per_device) + summed.shape[1:])
    arrived = lax.all_to_all(reduced, KA, split_axis=0, concat_axis=3, tiled=True)
    k_field = arrived.reshape(per_device, 5, width, 2, width)
    position = lax.axis_index(KA) * row_size + lax.axis_index(ROW)
    own_weight = lax.dynamic_slice_in_dim(weight, position * per_device, per_device)
    return curvature(k_field, eigvecs, occupied, own_weight)


def solution(mesh):
    finer = Mesh(mesh.devices.reshape(4, 4, 4, 2), ("ka_0", "ka_1", "row_0", "row_1"))
    placed = (
        P(KA, None),
        P(KA),
        P(KA_ROW),
        P(ROW, None),
        P(ROW, None, KA, None, None),
        P(KA_ROW, None, None, None),
        P(KA_ROW, None),
    )
    return jax.shard_map(
        on_device, mesh=finer, in_specs=placed, out_specs=P(KA_ROW), check_vma=False
    )
```

profile of v0, /device:TPU:83, one launch (start us, length us, event | category | flops | bytes accessed | tf_op | source)
XLA Modules:
  0.0 414.8 jit_solution(16123658147926405169)
XLA Ops:
  6.5 1.3 broadcast_in_dim.73
  7.8 6.8 %all-to-all-start = ((s32[16,1,8]{2,1,0:T(1,128)}), s32[16,1,8]{2,1,0:T(1,128)S(1)}, u32[]{:S(2)}, u32[]{:S(2)}) async-start(s32[16,1,8]{2,1,0:T(1,128)} %broadcast_in_dim.73), calls=%async_computation | async-start | bytes 16384 | tf_op jit(solution)/shard_map/all_to_all | solution.py:18
  14.7 7.2 %slice.203 = bf16[512,2,8,2,128]{4,3,2,1,0:T(2,128)(2,1)} slice(bf16[512,3,8,2,128]{4,3,2,1,0:T(2,128)(2,1)} %param.12), slice={[0:512], [1:3], [0:8], [0:2], [0:128]} | slice | bytes 8388608 | tf_op jit(solution)/shard_map/slice | solution.py:91
  23.1 0.8 dynamic-update-slice
  23.9 13.2 %all-reduce = s32[64]{0:T(128)S(1)} all-reduce(s32[64]{0:T(128)S(1)} %dynamic-update-slice), channel_id=2, replica_groups=mesh['ka_0'=4,'ka_1'=4,'row_0'=4,'row_1'=2] {'ka_0','ka_1','row_0'}, use_global_device_ids=true, to_apply=%add | all-reduce | flops 64 | bytes 512
  38.6 7.9 %all-reduce.1 = s32[128]{0:T(128)S(1)} all-reduce(s32[128]{0:T(128)S(1)} %dynamic-update-slice.1), channel_id=3, replica_groups=mesh['ka_0'=4,'ka_1'=4,'row_0'=4,'row_1'=2] {'row_1'}, use_global_device_ids=true, to_apply=%add.1 | all-reduce | flops 128 | bytes 1024
  47.2 2.8 reshape_squeeze.3
  50.0 11.2 %copy.186 = bf16[512,2,8,2,128]{0,4,3,2,1:T(8,128)(2,1)} copy(bf16[512,2,8,2,128]{4,3,2,1,0:T(2,128)(2,1)} %slice.203) | data formatting | bytes 8388608 | tf_op jit(solution)/shard_map/reshape | solution.py:91
  61.8 7.8 %all-to-all-start.1 = ((f32[16,8,3]{1,2,0:T(4,128)}), f32[16,8,3]{1,2,0:T(4,128)S(1)}, u32[]{:S(2)}, u32[]{:S(2)}) async-start(f32[16,8,3]{1,2,0:T(4,128)} %broadcast_in_dim.80), calls=%async_computation.1 | async-start | bytes 65536 | tf_op jit(solution)/shard_map/all_to_all | solution.py:18
  71.4 1.4 all-to-all-done.1
  73.4 1.5 gather_fusion
  75.3 4.3 %constant_dynamic-update-slice_fusion.1 = bf16[6,512,512]{2,1,0:T(8,128)(2,1)S(1)} fusion(f32[512]{0:T(512)S(1)} %bitcast.236, f32[512]{0:T(512)S(1)} %get-tuple-element.7, f32[512]{0:T(512)S(1)} %bitcast.229, f32[512]{0:T(512)S(1)} %get-tuple-element.6, f32[512]{0:T(512)S(1)} %bitcast.221, f32[512]{0:T(512)S(1)} %get-tuple-element.5), kind=kLoop, calls=%fused_computation.115 | loop fusion | flops 1835007 | bytes 536576
  79.7 5.7 %fusion.20 = (bf16[1,512,512]{2,1,0:T(8,128)(2,1)}, bf16[1,512,512]{2,1,0:T(8,128)(2,1)}) fusion(f32[512]{0:T(512)S(1)} %bitcast.237, f32[512]{0:T(512)S(1)} %get-tuple-element.7, f32[512]{0:T(512)S(1)} %bitcast.230, f32[512]{0:T(512)S(1)} %get-tuple-element.6, f32[512]{0:T(512)S(1)} %bitcast.222, f32[512]{0:T(512)S(1)} %get-tuple-element.5), kind=kLoop, calls=%fused_computation.47 | loop fusion | flops 2097152 | bytes 1060864 | tf_op jit(solution)/shard_map/convert
  85.3 4.3 %constant_dynamic-update-slice_fusion = bf16[6,512,512]{2,1,0:T(8,128)(2,1)S(1)} fusion(bf16[6,512,512]{2,1,0:T(8,128)(2,1)S(1)} %constant_dynamic-update-slice_fusion.1, f32[512]{0:T(512)S(1)} %bitcast.238, f32[512]{0:T(512)S(1)} %get-tuple-element.7, f32[512]{0:T(512)S(1)} %bitcast.231, f32[512]{0:T(512)S(1)} %get-tuple-element.6, f32[512]{0:T(512)S(1)} %bitcast.223, ...), kind=kLoop, calls=%fused_computation.114 | loop fusion | flops 1835008 | bytes 536576
  89.7 4.3 %fusion.22 = bf16[6,512,512]{2,1,0:T(8,128)(2,1)S(1)} fusion(bf16[6,512,512]{2,1,0:T(8,128)(2,1)S(1)} %constant_dynamic-update-slice_fusion, f32[512]{0:T(512)S(1)} %neg.16, f32[512]{0:T(512)S(1)} %bitcast.239, f32[512]{0:T(512)S(1)} %get-tuple-element.7, f32[512]{0:T(512)S(1)} %bitcast.232, f32[512]{0:T(512)S(1)} %get-tuple-element.6, f32[512]{0:T(512)S(1)} %bitcast.224, ...), kind=kLoop, calls=%fused_computation.49 | loop fusion | flops 2097152 | bytes 538624
  94.0 4.3 %fusion.23 = bf16[6,512,512]{2,1,0:T(8,128)(2,1)S(1)} fusion(bf16[6,512,512]{2,1,0:T(8,128)(2,1)S(1)} %fusion.22, f32[512]{0:T(512)S(1)} %bitcast.240, f32[512]{0:T(512)S(1)} %get-tuple-element.7, f32[512]{0:T(512)S(1)} %bitcast.233, f32[512]{0:T(512)S(1)} %get-tuple-element.6, f32[512]{0:T(512)S(1)} %bitcast.225, f32[512]{0:T(512)S(1)} %get-tuple-element.5), kind=kLoop, calls=%fused_computation.50 | loop fusion | flops 2097152 | bytes 536576
  98.3 4.3 %fusion.24 = bf16[6,512,512]{2,1,0:T(8,128)(2,1)S(1)} fusion(bf16[6,512,512]{2,1,0:T(8,128)(2,1)S(1)} %fusion.23, f32[512]{0:T(512)S(1)} %neg.17, f32[512]{0:T(512)S(1)} %bitcast.241, f32[512]{0:T(512)S(1)} %get-tuple-element.7, f32[512]{0:T(512)S(1)} %bitcast.234, f32[512]{0:T(512)S(1)} %get-tuple-element.6, f32[512]{0:T(512)S(1)} %bitcast.226, ...), kind=kLoop, calls=%fused_computation.51 | loop fusion | flops 2097152 | bytes 538624
  102.7 4.3 %fusion.25 = bf16[6,512,512]{2,1,0:T(8,128)(2,1)S(1)} fusion(bf16[6,512,512]{2,1,0:T(8,128)(2,1)S(1)} %fusion.24, f32[512]{0:T(512)S(1)} %bitcast.242, f32[512]{0:T(512)S(1)} %get-tuple-element.7, f32[512]{0:T(512)S(1)} %bitcast.235, f32[512]{0:T(512)S(1)} %get-tuple-element.6, f32[512]{0:T(512)S(1)} %bitcast.227, f32[512]{0:T(512)S(1)} %get-tuple-element.5), kind=kLoop, calls=%fused_computation.52 | loop fusion | flops 2097152 | bytes 536576 | tf_op jit(solution)/shard_map/stack | solution.py:73
  107.0 11.9 %fusion.73 = f32[3072,2048]{0,1:T(8,128)} fusion(bf16[3072,512]{1,0:T(8,128)(2,1)S(1)} %bitcast.243, bf16[512,2048]{1,0:T(8,128)(2,1)S(1)} %copy-done.12), kind=kOutput, calls=%fused_computation.133 | convolution fusion | flops 6442450944 | bytes 30408704 | tf_op jit(solution)/shard_map/dot_general | solution.py:92
  118.9 16.1 %fusion.65 = (f32[512,2048]{0,1:T(8,128)}, f32[512,2048]{0,1:T(8,128)}, f32[512,2048]{0,1:T(8,128)}, f32[512,2048]{0,1:T(8,128)}, f32[512,2048]{0,1:T(8,128)S(1)}, /*index=5*/f32[512,2048]{0,1:T(8,128)}) fusion(f32[3072,2048]{0,1:T(8,128)} %fusion.73), kind=kLoop, calls=%fused_computation.125 | loop fusion | bytes 50331648 | tf_op jit(solution)/shard_map/slice | solution.py:103
  135.0 1.8 fusion.70
  136.7 2.9 copy.191
  139.6 4.8 %fusion.71 = (f32[512,8,1,128]{0,3,2,1:T(8,128)}, f32[512,8,1,128]{0,3,2,1:T(8,128)}) fusion(f32[512,8,2,128]{0,3,2,1:T(8,128)} %bitcast.215), kind=kLoop, calls=%fused_computation.131 | loop fusion | bytes 8388608 | tf_op jit(solution)/shard_map/slice | solution.py:79
  144.5 2.9 copy.192
  147.4 2.9 copy.189
  150.3 1.8 copy.190
  152.1 4.2 %fusion.68 = (f32[512,8,1,128]{0,3,2,1:T(8,128)S(1)}, f32[512,8,1,128]{0,3,2,1:T(8,128)}) fusion(f32[512,8,2,128]{0,3,2,1:T(8,128)} %bitcast.214), kind=kLoop, calls=%fused_computation.128 | loop fusion | bytes 8388608 | tf_op jit(solution)/shard_map/slice | solution.py:79
  156.4 3.0 copy.195
  159.3 4.8 %fusion.69 = (f32[512,8,1,128]{0,3,2,1:T(8,128)}, f32[512,8,1,128]{0,3,2,1:T(8,128)}) fusion(f32[512,8,2,128]{0,3,2,1:T(8,128)} %bitcast.213), kind=kLoop, calls=%fused_computation.129 | loop fusion | bytes 8388608 | tf_op jit(solution)/shard_map/slice | solution.py:79
  164.1 2.9 copy.196
  167.0 2.9 copy.193
  169.9 1.8 copy.194
  171.7 4.2 %fusion.66 = (f32[512,8,1,128]{0,3,2,1:T(8,128)S(1)}, f32[512,8,1,128]{0,3,2,1:T(8,128)}) fusion(f32[512,8,2,128]{0,3,2,1:T(8,128)} %bitcast.212), kind=kLoop, calls=%fused_computation.126 | loop fusion | bytes 8388608 | tf_op jit(solution)/shard_map/slice | solution.py:79
  175.9 2.9 copy.199
  178.8 4.8 %fusion.67 = (f32[512,8,1,128]{0,3,2,1:T(8,128)}, f32[512,8,1,128]{0,3,2,1:T(8,128)}) fusion(f32[512,8,2,128]{0,3,2,1:T(8,128)} %bitcast.211), kind=kLoop, calls=%fused_computation.127 | loop fusion | bytes 8388608 | tf_op jit(solution)/shard_map/slice | solution.py:79
  183.6 2.9 copy.200
  186.6 2.9 copy.197
  189.5 1.8 copy.198
  191.3 6.4 %fusion.5 = f32[2,512,2,8,2,128]{5,1,4,3,2,0:T(8,128)S(1)} fusion(bf16[512,2,8,2,128]{0,4,3,2,1:T(8,128)(2,1)} %copy.186, bf16[1,512,512]{2,1,0:T(8,128)(2,1)S(1)} %copy-done.14, bf16[1,512,512]{2,1,0:T(8,128)(2,1)S(1)} %copy-done.13), kind=kOutput, calls=%fused_computation.15 | convolution fusion | flops 4297064448 | bytes 22020096 | tf_op jit(solution)/shard_map/dot_general | solution.py:95
  197.7 4.8 %slice_bitcast_fusion = (f32[512,8,2,128]{3,0,2,1:T(8,128)S(1)}, f32[512,8,2,128]{3,0,2,1:T(8,128)}, f32[512,8,2,128]{3,0,2,1:T(8,128)}, f32[512,8,2,128]{3,0,2,1:T(8,128)}) fusion(f32[2,512,2,8,2,128]{5,1,4,3,2,0:T(8,128)S(1)} %fusion.5), kind=kLoop, calls=%fused_computation.1 | loop fusion | bytes 33554432 | tf_op jit(solution)/shard_map/squeeze | solution.py:105
  202.5 2.6 add.198
  206.2 2.4 fusion
  208.6 1.3 copy-done.3
  210.1 1.4 copy-done.4
  212.3 1.4 copy-done.6
  214.6 1.4 copy-done.8
  216.8 2.3 fusion.1
  219.0 2.3 fusion.2
  221.3 8.4 %slice_subtract_fusion = (f32[512,8,1,128]{3,0,2,1:T(8,128)}, f32[512,8,1,128]{3,0,2,1:T(8,128)}, f32[512,8,1,128]{3,0,2,1:T(8,128)}, f32[512,8,1,128]{3,0,2,1:T(8,128)}) fusion(f32[512,8,2,128]{3,0,2,1:T(8,128)S(1)} %get-tuple-element.14, f32[512,8,2,128]{3,0,2,1:T(8,128)} %get-tuple-element.15, f32[512,8,2,128]{3,0,2,1:T(8,128)} %get-tuple-element.17, ...), kind=kLoop, calls=%fused_computation.19 | loop fusion | flops 2097152 | bytes 25165824 | tf_op jit(solution)/shard_map/sub | solution.py:79
  229.7 4.7 %fusion.3 = f32[512,5,8,2,128]{4,0,3,2,1:T(8,128)} fusion(f32[512,5,8,2,128]{4,0,3,2,1:T(8,128)} %fusion.2, f32[512,8,1,128]{3,0,2,1:T(8,128)} %get-tuple-element.45, f32[512,8,1,128]{3,0,2,1:T(8,128)} %get-tuple-element.46), kind=kLoop, calls=%fused_computation.12 | loop fusion | flops 1048576 | bytes 8388608
  234.4 2.2 fusion.4
  236.6 111.7 %reduce-scatter.2.cloned.1.call-done = f32[64,5,8,2,128]{4,0,3,2,1:T(8,128)} async-done(((f32[512,5,8,2,128]{4,0,3,2,1:T(8,128)}), f32[64,5,8,2,128]{4,0,3,2,1:T(8,128)}) %reduce-scatter.2.cloned.1.call-update) | async-done | bytes 2621456 | tf_op jit(solution)/shard_map/reduce_scatter | solution.py:165
  348.3 4.0 copy.155
  352.3 6.8 %all-to-all-start.2 = ((f32[16,4,5,8,2,128]{5,1,4,3,2,0:T(4,128)}), f32[16,4,5,8,2,128]{5,1,4,3,2,0:T(4,128)S(1)}, u32[]{:S(2)}, u32[]{:S(2)}) async-start(f32[16,4,5,8,2,128]{5,1,4,3,2,0:T(4,128)} %copy.155), calls=%async_computation.3 | async-start | bytes 5242880 | tf_op jit(solution)/shard_map/all_to_all | solution.py:169
  359.2 1.0 copy_convert_fusion
  360.4 37.9 %all-to-all-done.2 = f32[16,4,5,8,2,128]{5,1,4,3,2,0:T(4,128)S(1)} async-done(((f32[16,4,5,8,2,128]{5,1,4,3,2,0:T(4,128)}), f32[16,4,5,8,2,128]{5,1,4,3,2,0:T(4,128)S(1)}, u32[]{:S(2)}, u32[]{:S(2)}) %all-to-all-start.2) | async-done | bytes 2621472 | tf_op jit(solution)/shard_map/all_to_all | solution.py:169
  399.2 0.7 fusion.47
  399.9 0.7 fusion.10
  400.7 0.8 convolution_add_fusion
  401.4 1.0 fusion.16
  402.4 0.8 convolution_subtract_fusion
  403.2 1.0 fusion.14
  404.3 1.0 fusion.8
  405.4 1.0 fusion.7
  (97 shorter events, 11.7 us)
Async XLA Ops:
  7.8 53.4 %all-to-all-start = ((s32[16,1,8]{2,1,0:T(1,128)}), s32[16,1,8]{2,1,0:T(1,128)S(1)}, u32[]{:S(2)}, u32[]{:S(2)}) async-start(s32[16,1,8]{2,1,0:T(1,128)} %broadcast_in_dim.73), calls=%async_computation | async-start | bytes 16384 | tf_op jit(solution)/shard_map/all_to_all | solution.py:18
  14.6 7.2 %copy-start.15 = (s32[512,3]{0,1:T(4,128)S(1)}, s32[512,3]{0,1:T(4,128)}, u32[]{:S(2)}) copy-start(s32[512,3]{0,1:T(4,128)} %param.11) | copy-start | bytes 18436
  14.7 7.9 %copy-start.20 = (u32[128]{0:T(128)S(1)}, u32[128]{0:T(128)}, u32[]{:S(2)}) copy-start(u32[128]{0:T(128)} %constant.56) | copy-start | bytes 1540
  14.7 22.5 %copy-start.19 = (u32[128]{0:T(128)S(1)}, u32[128]{0:T(128)}, u32[]{:S(2)}) copy-start(u32[128]{0:T(128)} %constant.61) | copy-start | bytes 1540
  14.7 32.5 %slice-start = ((bf16[512,3,8,2,128]{4,3,2,1,0:T(2,128)(2,1)}), bf16[512,1,8,2,128]{4,3,2,1,0:T(2,128)(2,1)S(1)}, s32[]{:S(2)}) async-start(bf16[512,3,8,2,128]{4,3,2,1,0:T(2,128)(2,1)} %param.12), calls=%async_computation.5 | async-start | bytes 4194304 | tf_op jit(solution)/shard_map/slice | solution.py:90
  50.0 11.2 %copy-start.17 = (f32[8,3]{0,1:T(4,128)S(1)}, f32[8,3]{0,1:T(4,128)}, u32[]{:S(2)}) copy-start(f32[8,3]{0,1:T(4,128)} %param.8) | copy-start | bytes 292
  50.0 23.2 %copy-start.18 = (f32[3]{0:T(128)S(1)}, f32[3]{0:T(128)}, u32[]{:S(2)}) copy-start(f32[3]{0:T(128)} %constant.47.clone) | copy-start | bytes 40
  61.8 11.0 %all-to-all-start.1 = ((f32[16,8,3]{1,2,0:T(4,128)}), f32[16,8,3]{1,2,0:T(4,128)S(1)}, u32[]{:S(2)}, u32[]{:S(2)}) async-start(f32[16,8,3]{1,2,0:T(4,128)} %broadcast_in_dim.80), calls=%async_computation.1 | async-start | bytes 65536 | tf_op jit(solution)/shard_map/all_to_all | solution.py:18
  69.7 278.7 %reduce-scatter.2.cloned.1.call-start = ((), (), s32[]{:S(2)}) async-start(), calls=%async_computation.4 | async-start | bytes 23592960 | tf_op jit(solution)/shard_map/reduce_scatter | solution.py:165
  75.3 31.7 %copy-start.12 = (bf16[512,2048]{1,0:T(8,128)(2,1)S(1)}, bf16[512,2048]{1,0:T(8,128)(2,1)}, u32[]{:S(2)}) copy-start(bf16[512,2048]{1,0:T(8,128)(2,1)} %reshape_squeeze.3) | copy-start | bytes 6291460
  189.5 1.8 copy-start.13
  189.5 1.8 copy-start.14
  202.5 2.9 copy-start
  202.5 3.5 copy-start.1
  206.2 2.4 copy-start.2
  206.2 3.7 copy-start.3
  209.9 1.6 copy-start.4
  209.9 2.2 copy-start.5
  212.1 1.6 copy-start.6
  212.1 2.2 copy-start.7
  214.3 1.6 copy-start.8
  214.4 2.2 copy-start.9
  229.7 4.7 %copy-start.10 = (f32[512,8,1,128]{3,0,2,1:T(8,128)S(1)}, f32[512,8,1,128]{3,0,2,1:T(8,128)}, u32[]{:S(2)}) copy-start(f32[512,8,1,128]{3,0,2,1:T(8,128)} %get-tuple-element.18) | copy-start | bytes 6291460
  229.7 4.7 %copy-start.11 = (f32[512,8,1,128]{3,0,2,1:T(8,128)S(1)}, f32[512,8,1,128]{3,0,2,1:T(8,128)}, u32[]{:S(2)}) copy-start(f32[512,8,1,128]{3,0,2,1:T(8,128)} %get-tuple-element.19) | copy-start | bytes 6291460
  352.3 6.8 %copy-start.16 = (s32[4,128]{1,0:T(4,128)S(1)}, s32[4,128]{1,0:T(4,128)}, u32[]{:S(2)}) copy-start(s32[4,128]{1,0:T(4,128)} %param.14) | copy-start | bytes 6148
  352.3 46.0 %all-to-all-start.2 = ((f32[16,4,5,8,2,128]{5,1,4,3,2,0:T(4,128)}), f32[16,4,5,8,2,128]{5,1,4,3,2,0:T(4,128)S(1)}, u32[]{:S(2)}, u32[]{:S(2)}) async-start(f32[16,4,5,8,2,128]{5,1,4,3,2,0:T(4,128)} %copy.155), calls=%async_computation.3 | async-start | bytes 5242880 | tf_op jit(solution)/shard_map/all_to_all | solution.py:169
Sparse Core Ops, SparseCore 0:
  236.8 111.5 reduce-scatter.1
where the time goes:
time: 420 us; the launch traced here: 415 us
  waiting for transfers between devices  151 us (36%)
  local copies, waits for them, and re-layouts  119 us (28%)
  other arithmetic  61 us (15%)
  matrix products  25.3 us (6%)
  starting transfers between devices  21.5 us (5%)
  blocking collectives  21.1 us (5%)
  between operations  15.4 us (4%)
    reduce_scatter x1, waiting for transfers between devices, on_device(): lax.psum_scatter(fourier(kpoints[slot_order], lattice, real_space), ROW,...  112 us
    unnamed x60, local copies, waits for them, and re-layouts  42.1 us
    all_to_all x1, waiting for transfers between devices, on_device(): lax.all_to_all(reduced, KA, split_axis=0, concat_axis=3, tiled=True)  37.9 us
    unnamed x9, other arithmetic  33.3 us
    slice x6, local copies, waits for them, and re-layouts, combine(): real_part = first_part[..., 0, :] - second_part[..., 1, :]  24.6 us
    unnamed x2, blocking collectives  21.1 us
    slice x1, local copies, waits for them, and re-layouts, fourier(): product_h[4]  16.1 us
    all_to_all x2, starting transfers between devices, sent_to_all(): return lax.all_to_all(copies, axis, split_axis=0, concat_axis=0, tiled=True)  14.7 us
  transfers between devices with their start and end apart: 4, of which 3 were waited for; matrix products, arithmetic and copies ran while one was open for 6% of the time, Pallas kernels for 0%

commit v1 on v0

--- a/solution.py
+++ b/solution.py
@@ -166,7 +166,9 @@
         fourier(kpoints[slot_order], lattice, real_space), ROW, scatter_dimension=0, tiled=True
     )
     reduced = summed.reshape((ka_size, per_device) + summed.shape[1:])
-    arrived = lax.all_to_all(reduced, KA, split_axis=0, concat_axis=3, tiled=True)
+    arrived = jnp.concatenate(
+        lax.all_to_all(jnp.stack(jnp.split(reduced, lax.axis_size(KA), axis=0)), KA, 0, 0), axis=3
+    )
     k_field = arrived.reshape(per_device, 5, width, 2, width)
     position = lax.axis_index(KA) * row_size + lax.axis_index(ROW)
     own_weight = lax.dynamic_slice_in_dim(weight, position * per_device, per_device)

time: 420 us -> 444 us (1.057)
  local copies, waits for them, and re-layouts: 119 us -> 142 us
    unnamed x60 -> x75, local copies, waits for them, and re-layouts: 42.1 us -> 67 us
where the time goes in v1:
time: 444 us; the launch traced here: 437 us
  waiting for transfers between devices  151 us (34%)
  local copies, waits for them, and re-layouts  142 us (32%)
  other arithmetic  61 us (14%)
  matrix products  25.3 us (6%)
  starting transfers between devices  21.5 us (5%)
  blocking collectives  21.1 us (5%)
  between operations  15.5 us (3%)
    reduce_scatter x1, waiting for transfers between devices, on_device(): lax.psum_scatter(fourier(kpoints[slot_order], lattice, real_space), ROW,...  112 us
    unnamed x75, local copies, waits for them, and re-layouts  67 us
    all_to_all x1, waiting for transfers between devices, on_device(): lax.all_to_all(jnp.stack(jnp.split(reduced, lax.axis_size(KA), axis=0)),...  37.9 us
    unnamed x9, other arithmetic  33.3 us
    slice x6, local copies, waits for them, and re-layouts, combine(): real_part = first_part[..., 0, :] - second_part[..., 1, :]  24.6 us
    unnamed x2, blocking collectives  21.1 us
    slice x1, local copies, waits for them, and re-layouts, fourier(): product_h[4]  16.1 us
    all_to_all x2, starting transfers between devices, sent_to_all(): return lax.all_to_all(copies, axis, split_axis=0, concat_axis=0, tiled=True)  14.7 us
  transfers between devices with their start and end apart: 4, of which 3 were waited for; matrix products, arithmetic and copies ran while one was open for 6% of the time, Pallas kernels for 0%

profile of v1, /device:TPU:83, one launch (start us, length us, event | category | flops | bytes accessed | tf_op | source)
XLA Modules:
  0.0 437.5 jit_solution(16898575967570664315)
XLA Ops:
  7.8 6.8 %all-to-all-start = ((s32[16,1,8]{2,1,0:T(1,128)}), s32[16,1,8]{2,1,0:T(1,128)S(1)}, u32[]{:S(2)}, u32[]{:S(2)}) async-start(s32[16,1,8]{2,1,0:T(1,128)} %broadcast_in_dim.73), calls=%async_computation | async-start | bytes 16384 | tf_op jit(solution)/shard_map/all_to_all | solution.py:18
  14.7 7.2 %slice.219 = bf16[512,2,8,2,128]{4,3,2,1,0:T(2,128)(2,1)} slice(bf16[512,3,8,2,128]{4,3,2,1,0:T(2,128)(2,1)} %param.12), slice={[0:512], [1:3], [0:8], [0:2], [0:128]} | slice | bytes 8388608 | tf_op jit(solution)/shard_map/slice | solution.py:91
  23.9 13.2 %all-reduce = s32[64]{0:T(128)S(1)} all-reduce(s32[64]{0:T(128)S(1)} %dynamic-update-slice), channel_id=2, replica_groups=mesh['ka_0'=4,'ka_1'=4,'row_0'=4,'row_1'=2] {'ka_0','ka_1','row_0'}, use_global_device_ids=true, to_apply=%add | all-reduce | flops 64 | bytes 512
  38.6 7.9 %all-reduce.1 = s32[128]{0:T(128)S(1)} all-reduce(s32[128]{0:T(128)S(1)} %dynamic-update-slice.1), channel_id=3, replica_groups=mesh['ka_0'=4,'ka_1'=4,'row_0'=4,'row_1'=2] {'row_1'}, use_global_device_ids=true, to_apply=%add.1 | all-reduce | flops 128 | bytes 1024
  47.2 2.8 reshape_squeeze.3
  50.0 11.2 %copy.190 = bf16[512,2,8,2,128]{0,4,3,2,1:T(8,128)(2,1)} copy(bf16[512,2,8,2,128]{4,3,2,1,0:T(2,128)(2,1)} %slice.219) | data formatting | bytes 8388608 | tf_op jit(solution)/shard_map/reshape | solution.py:91
  61.8 7.8 %all-to-all-start.1 = ((f32[16,8,3]{1,2,0:T(4,128)}), f32[16,8,3]{1,2,0:T(4,128)S(1)}, u32[]{:S(2)}, u32[]{:S(2)}) async-start(f32[16,8,3]{1,2,0:T(4,128)} %broadcast_in_dim.80), calls=%async_computation.1 | async-start | bytes 65536 | tf_op jit(solution)/shard_map/all_to_all | solution.py:18
  71.4 1.4 all-to-all-done.1
  73.4 1.5 gather_fusion
  75.3 4.3 constant_dynamic-update-slice_fusion.1
  79.7 5.7 %fusion.20 = (bf16[1,512,512]{2,1,0:T(8,128)(2,1)}, bf16[1,512,512]{2,1,0:T(8,128)(2,1)}) fusion(f32[512]{0:T(512)S(1)} %bitcast.299, f32[512]{0:T(512)S(1)} %get-tuple-element.7, f32[512]{0:T(512)S(1)} %bitcast.292, f32[512]{0:T(512)S(1)} %get-tuple-element.6, f32[512]{0:T(512)S(1)} %bitcast.284, f32[512]{0:T(512)S(1)} %get-tuple-element.5), kind=kLoop, calls=%fused_computation.47 | loop fusion | flops 2097152 | bytes 1060864 | tf_op jit(solution)/shard_map/convert
  85.3 4.3 constant_dynamic-update-slice_fusion
  89.7 4.3 fusion.22
  94.0 4.3 fusion.23
  98.3 4.3 fusion.24
  102.7 4.3 fusion.25
  107.0 11.9 %fusion.89 = f32[3072,2048]{0,1:T(8,128)} fusion(bf16[3072,512]{1,0:T(8,128)(2,1)S(1)} %bitcast.305, bf16[512,2048]{1,0:T(8,128)(2,1)S(1)} %copy-done.12), kind=kOutput, calls=%fused_computation.165 | convolution fusion | flops 6442450944 | bytes 30408704 | tf_op jit(solution)/shard_map/dot_general | solution.py:92
  118.9 16.1 %fusion.81 = (f32[512,2048]{0,1:T(8,128)}, f32[512,2048]{0,1:T(8,128)}, f32[512,2048]{0,1:T(8,128)}, f32[512,2048]{0,1:T(8,128)}, f32[512,2048]{0,1:T(8,128)S(1)}, /*index=5*/f32[512,2048]{0,1:T(8,128)}) fusion(f32[3072,2048]{0,1:T(8,128)} %fusion.89), kind=kLoop, calls=%fused_computation.157 | loop fusion | bytes 50331648 | tf_op jit(solution)/shard_map/slice | solution.py:103
  135.0 1.8 fusion.86
  136.7 2.9 copy.197
  139.6 4.8 %fusion.87 = (f32[512,8,1,128]{0,3,2,1:T(8,128)}, f32[512,8,1,128]{0,3,2,1:T(8,128)}) fusion(f32[512,8,2,128]{0,3,2,1:T(8,128)} %bitcast.278), kind=kLoop, calls=%fused_computation.163 | loop fusion | bytes 8388608 | tf_op jit(solution)/shard_map/slice | solution.py:79
  144.5 2.9 copy.198
  147.4 2.9 copy.195
  150.3 1.8 copy.196
  152.1 4.2 fusion.84
  156.4 3.0 copy.201
  159.3 4.8 %fusion.85 = (f32[512,8,1,128]{0,3,2,1:T(8,128)}, f32[512,8,1,128]{0,3,2,1:T(8,128)}) fusion(f32[512,8,2,128]{0,3,2,1:T(8,128)} %bitcast.276), kind=kLoop, calls=%fused_computation.161 | loop fusion | bytes 8388608 | tf_op jit(solution)/shard_map/slice | solution.py:79
  164.1 2.9 copy.202
  167.0 2.9 copy.199
  169.9 1.8 copy.200
  171.7 4.2 fusion.82
  175.9 2.9 copy.205
  178.8 4.8 %fusion.83 = (f32[512,8,1,128]{0,3,2,1:T(8,128)}, f32[512,8,1,128]{0,3,2,1:T(8,128)}) fusion(f32[512,8,2,128]{0,3,2,1:T(8,128)} %bitcast.274), kind=kLoop, calls=%fused_computation.159 | loop fusion | bytes 8388608 | tf_op jit(solution)/shard_map/slice | solution.py:79
  183.6 2.9 copy.206
  186.6 2.9 copy.203
  189.5 1.8 copy.204
  191.3 6.4 %fusion.5 = f32[2,512,2,8,2,128]{5,1,4,3,2,0:T(8,128)S(1)} fusion(bf16[512,2,8,2,128]{0,4,3,2,1:T(8,128)(2,1)} %copy.190, bf16[1,512,512]{2,1,0:T(8,128)(2,1)S(1)} %copy-done.14, bf16[1,512,512]{2,1,0:T(8,128)(2,1)S(1)} %copy-done.13), kind=kOutput, calls=%fused_computation.15 | convolution fusion | flops 4297064448 | bytes 22020096 | tf_op jit(solution)/shard_map/dot_general | solution.py:95
  197.7 4.8 %slice_bitcast_fusion = (f32[512,8,2,128]{3,0,2,1:T(8,128)S(1)}, f32[512,8,2,128]{3,0,2,1:T(8,128)}, f32[512,8,2,128]{3,0,2,1:T(8,128)}, f32[512,8,2,128]{3,0,2,1:T(8,128)}) fusion(f32[2,512,2,8,2,128]{5,1,4,3,2,0:T(8,128)S(1)} %fusion.5), kind=kLoop, calls=%fused_computation.1 | loop fusion | bytes 33554432 | tf_op jit(solution)/shard_map/squeeze | solution.py:105
  202.5 2.6 add.198
  206.2 2.4 fusion
  216.8 2.3 fusion.1
  219.0 2.3 fusion.2
  221.3 8.4 %slice_subtract_fusion = (f32[512,8,1,128]{3,0,2,1:T(8,128)}, f32[512,8,1,128]{3,0,2,1:T(8,128)}, f32[512,8,1,128]{3,0,2,1:T(8,128)}, f32[512,8,1,128]{3,0,2,1:T(8,128)}) fusion(f32[512,8,2,128]{3,0,2,1:T(8,128)S(1)} %get-tuple-element.14, f32[512,8,2,128]{3,0,2,1:T(8,128)} %get-tuple-element.15, f32[512,8,2,128]{3,0,2,1:T(8,128)} %get-tuple-element.17, ...), kind=kLoop, calls=%fused_computation.19 | loop fusion | flops 2097152 | bytes 25165824 | tf_op jit(solution)/shard_map/sub | solution.py:79
  229.7 4.7 %fusion.3 = f32[512,5,8,2,128]{4,0,3,2,1:T(8,128)} fusion(f32[512,5,8,2,128]{4,0,3,2,1:T(8,128)} %fusion.2, f32[512,8,1,128]{3,0,2,1:T(8,128)} %get-tuple-element.45, f32[512,8,1,128]{3,0,2,1:T(8,128)} %get-tuple-element.46), kind=kLoop, calls=%fused_computation.12 | loop fusion | flops 1048576 | bytes 8388608
  234.4 2.2 fusion.4
  236.6 111.7 %reduce-scatter.2.cloned.1.call-done = f32[64,5,8,2,128]{4,0,3,2,1:T(8,128)} async-done(((f32[512,5,8,2,128]{4,0,3,2,1:T(8,128)}), f32[64,5,8,2,128]{4,0,3,2,1:T(8,128)}) %reduce-scatter.2.cloned.1.call-update) | async-done | bytes 2621456 | tf_op jit(solution)/shard_map/reduce_scatter | solution.py:165
  348.3 1.7 fusion.61
  350.0 1.7 fusion.60
  351.7 1.6 fusion.59
  353.3 1.7 fusion.58
  355.0 1.7 fusion.57
  356.7 1.7 fusion.56
  358.3 1.7 fusion.55
  360.0 1.7 fusion.54
  361.7 1.6 fusion.53
  363.3 1.7 fusion.52
  365.0 1.7 fusion.51
  366.7 1.7 fusion.50
  368.4 1.7 fusion.49
  370.0 1.7 fusion.48
  371.7 1.6 fusion.47
  373.3 1.7 fusion.46
  375.0 6.8 %all-to-all-start.2 = ((f32[16,1,4,5,8,2,128]{6,2,5,4,3,1,0:T(4,128)}), f32[16,1,4,5,8,2,128]{6,2,5,4,3,1,0:T(4,128)S(1)}, u32[]{:S(2)}, u32[]{:S(2)}) async-start(f32[16,1,4,5,8,2,128]{6,2,5,4,3,1,0:T(4,128)} %fusion.46), calls=%async_computation.3 | async-start | bytes 5242880 | tf_op jit(solution)/shard_map/all_to_all | solution.py:170
  383.1 37.9 %all-to-all-done.2 = f32[16,1,4,5,8,2,128]{6,2,5,4,3,1,0:T(4,128)S(1)} async-done(((f32[16,1,4,5,8,2,128]{6,2,5,4,3,1,0:T(4,128)}), f32[16,1,4,5,8,2,128]{6,2,5,4,3,1,0:T(4,128)S(1)}, u32[]{:S(2)}, u32[]{:S(2)}) %all-to-all-start.2) | async-done | bytes 2621472 | tf_op jit(solution)/shard_map/all_to_all | solution.py:170
  (112 shorter events, 27.2 us)
Async XLA Ops:
  7.8 53.4 %all-to-all-start = ((s32[16,1,8]{2,1,0:T(1,128)}), s32[16,1,8]{2,1,0:T(1,128)S(1)}, u32[]{:S(2)}, u32[]{:S(2)}) async-start(s32[16,1,8]{2,1,0:T(1,128)} %broadcast_in_dim.73), calls=%async_computation | async-start | bytes 16384 | tf_op jit(solution)/shard_map/all_to_all | solution.py:18
  14.6 7.2 %copy-start.15 = (s32[512,3]{0,1:T(4,128)S(1)}, s32[512,3]{0,1:T(4,128)}, u32[]{:S(2)}) copy-start(s32[512,3]{0,1:T(4,128)} %param.11) | copy-start | bytes 18436
  14.7 7.9 %copy-start.20 = (u32[128]{0:T(128)S(1)}, u32[128]{0:T(128)}, u32[]{:S(2)}) copy-start(u32[128]{0:T(128)} %constant.56) | copy-start | bytes 1540
  14.7 22.5 %copy-start.19 = (u32[128]{0:T(128)S(1)}, u32[128]{0:T(128)}, u32[]{:S(2)}) copy-start(u32[128]{0:T(128)} %constant.61) | copy-start | bytes 1540
  14.7 32.5 %slice-start = ((bf16[512,3,8,2,128]{4,3,2,1,0:T(2,128)(2,1)}), bf16[512,1,8,2,128]{4,3,2,1,0:T(2,128)(2,1)S(1)}, s32[]{:S(2)}) async-start(bf16[512,3,8,2,128]{4,3,2,1,0:T(2,128)(2,1)} %param.12), calls=%async_computation.5 | async-start | bytes 4194304 | tf_op jit(solution)/shard_map/slice | solution.py:90
  50.0 11.2 %copy-start.17 = (f32[8,3]{0,1:T(4,128)S(1)}, f32[8,3]{0,1:T(4,128)}, u32[]{:S(2)}) copy-start(f32[8,3]{0,1:T(4,128)} %param.8) | copy-start | bytes 292
  50.0 23.2 %copy-start.18 = (f32[3]{0:T(128)S(1)}, f32[3]{0:T(128)}, u32[]{:S(2)}) copy-start(f32[3]{0:T(128)} %constant.47.clone) | copy-start | bytes 40
  61.8 11.0 %all-to-all-start.1 = ((f32[16,8,3]{1,2,0:T(4,128)}), f32[16,8,3]{1,2,0:T(4,128)S(1)}, u32[]{:S(2)}, u32[]{:S(2)}) async-start(f32[16,8,3]{1,2,0:T(4,128)} %broadcast_in_dim.80), calls=%async_computation.1 | async-start | bytes 65536 | tf_op jit(solution)/shard_map/all_to_all | solution.py:18
  69.7 278.7 %reduce-scatter.2.cloned.1.call-start = ((), (), s32[]{:S(2)}) async-start(), calls=%async_computation.4 | async-start | bytes 23592960 | tf_op jit(solution)/shard_map/reduce_scatter | solution.py:165
  74.9 32.1 %copy-start.12 = (bf16[512,2048]{1,0:T(8,128)(2,1)S(1)}, bf16[512,2048]{1,0:T(8,128)(2,1)}, u32[]{:S(2)}) copy-start(bf16[512,2048]{1,0:T(8,128)(2,1)} %reshape_squeeze.3) | copy-start | bytes 6291460
  189.5 1.8 copy-start.13
  189.5 1.8 copy-start.14
  202.5 2.9 copy-start
  202.5 3.5 copy-start.1
  206.2 2.4 copy-start.2
  206.2 3.7 copy-start.3
  209.9 1.6 copy-start.4
  209.9 2.2 copy-start.5
  212.1 1.6 copy-start.6
  212.1 2.2 copy-start.7
  214.3 1.6 copy-start.8
  214.4 2.2 copy-start.9
  229.7 4.7 %copy-start.10 = (f32[512,8,1,128]{3,0,2,1:T(8,128)S(1)}, f32[512,8,1,128]{3,0,2,1:T(8,128)}, u32[]{:S(2)}) copy-start(f32[512,8,1,128]{3,0,2,1:T(8,128)} %get-tuple-element.18) | copy-start | bytes 6291460
  229.7 4.7 %copy-start.11 = (f32[512,8,1,128]{3,0,2,1:T(8,128)S(1)}, f32[512,8,1,128]{3,0,2,1:T(8,128)}, u32[]{:S(2)}) copy-start(f32[512,8,1,128]{3,0,2,1:T(8,128)} %get-tuple-element.19) | copy-start | bytes 6291460
  375.0 6.8 %copy-start.16 = (s32[4,128]{1,0:T(4,128)S(1)}, s32[4,128]{1,0:T(4,128)}, u32[]{:S(2)}) copy-start(s32[4,128]{1,0:T(4,128)} %param.14) | copy-start | bytes 6148
  375.0 46.0 %all-to-all-start.2 = ((f32[16,1,4,5,8,2,128]{6,2,5,4,3,1,0:T(4,128)}), f32[16,1,4,5,8,2,128]{6,2,5,4,3,1,0:T(4,128)S(1)}, u32[]{:S(2)}, u32[]{:S(2)}) async-start(f32[16,1,4,5,8,2,128]{6,2,5,4,3,1,0:T(4,128)} %fusion.46), calls=%async_computation.3 | async-start | bytes 5242880 | tf_op jit(solution)/shard_map/all_to_all | solution.py:170
Sparse Core Ops, SparseCore 0:
  236.8 111.5 reduce-scatter.1
